TPU v7x, 256 devices: a 2x2x32 block of a 4x8x32 slice. The times are simulated.
256 devices in a mesh: parts: 4 (over x, y), row: 64 (over z, core).
Axes of the slice: x: 2, y: 2, z: 32, core: 2. Of those that a mesh axis runs over, the one named last changes fastest.
The devices are a block of a 4x8x32 slice.
Arguments:
- embeddings: bfloat16 [131072, 512], P(('parts', 'row')), parts along dimension 0, may hold values from -6 to 6
- sizes: int32 [512], P('parts'), parts along dimension 0, may hold values from 1 to 2048, 32768 in all
- order: int32 [131072], P('parts'), parts along dimension 0, may hold values from 0 to 32767, each once
Outputs:
- similarity: float32 [131072], P(('parts', 'row')), parts along dimension 0
There are 4 independent parts, one for each index of `parts`. A program takes and returns all parts, laid end to end along the dimension named above; each array names one. Nothing has to cross between parts.
Inputs may be any that keep to these rules, and one draw needn't show every extreme that they name: `sizes`: each cluster has 1 to 2048 items; they sum to 32768. `order`: each of 0 to 32767 once.
All inputs are finite; a program needn't handle non-finite values.
Results may differ from a plain program's by a relative error of at most 0.0014.
Values may be sent and summed in bfloat16 or wider, within the bound.
No kernel may reach another device: no remote copies, remote signals or barrier semaphores. Data moves between devices by JAX's collectives and lax.ppermute only.
A program may use at most 64 MiB of HBM per device.

v0:
```python
import functools

import jax
import jax.numpy as jnp
from jax import lax
from jax.experimental import pallas as pl
from jax.experimental.pallas import tpu as pltpu
from jax.sharding import PartitionSpec as P


STEP = 64
LANES = 128
BELOW, ABOVE = 2, 3
PIECES = BELOW + 1 + ABOVE


def moved(x, pairs):
    return lax.ppermute(x, "row", pairs)


def normalise(src, dst):
    for s in range(0, src.shape[0], STEP):
        v = src[s : s + STEP, :].astype(jnp.float32)
        v = v * lax.rsqrt(jnp.sum(v * v, axis=1, keepdims=True) + 1e-06)
        dst[s : s + STEP, :] = v.astype(jnp.bfloat16)


def key_rows(keys, piece):
    at = piece + BELOW
    return keys[at : at + 1, :], keys[8 + at : 9 + at, :]


def columns(key):
    return jnp.transpose(jnp.broadcast_to(key, (LANES, key.shape[1])))


def to_row(best):
    return jnp.max(jnp.transpose(best), axis=0, keepdims=True)


def score(x, y, out):
    out[...] = lax.dot_general(
        x[...], y[...], (((1,), (1,)), ((), ())), preferred_element_type=jnp.float32
    )


def pair_max(s, c1, c2, rows, rowbest=None):
    k1, k2 = rows
    n = k1.shape[1]
    over = [jnp.full((8, LANES), -1.0, jnp.float32) for _ in range(n // LANES)]
    for a in range(0, s.shape[0], STEP):
        x1, x2 = c1[a : a + STEP, :], c2[a : a + STEP, :]
        mine = None if rowbest is None else rowbest[a : a + STEP, :]
        for t in range(n // LANES):
            v = s[a : a + STEP, t * LANES : (t + 1) * LANES]
            y1, y2 = k1[:, t * LANES : (t + 1) * LANES], k2[:, t * LANES : (t + 1) * LANES]
            earlier = x1 < y1
            if rowbest is None:
                earlier = earlier & (x2 < y2)
            else:
                mine = jnp.maximum(mine, jnp.where(y2 < x2, v, -1.0))
            theirs = jnp.where(earlier, v, -1.0)
            over[t] = jnp.maximum(over[t], jnp.max(theirs.reshape(STEP // 8, 8, LANES), axis=0))
        if rowbest is not None:
            rowbest[a : a + STEP, :] = mine
    return jnp.concatenate([jnp.max(o, axis=0, keepdims=True) for o in over], axis=1)


def make_keys(sizes, order, keys, n, devices, me):
    clusters = sizes.shape[1]
    c = lax.broadcasted_iota(jnp.int32, (clusters, clusters), 0)
    k = lax.broadcasted_iota(jnp.int32, (clusters, clusters), 1)
    counted = jnp.where(k <= c, sizes[...].astype(jnp.float32), 0.0)
    ends = jnp.sum(counted, axis=1, keepdims=True)
    lane = lax.broadcasted_iota(jnp.int32, (1, n), 1)
    items = float(n * devices)
    rows = n // LANES
    for p in range(PIECES):
        place = me + (p - BELOW)
        index = (place * n + lane).astype(jnp.float32)
        cluster = jnp.sum(jnp.where(index >= ends, 1.0, 0.0), axis=0, keepdims=True)
        first = jnp.where(me == 1, 0, 1)
        cluster = jnp.where(place < first, -1.0, cluster) if p < BELOW else cluster
        at = jnp.clip(place, 0, devices - 1) * rows
        rank = jnp.concatenate([order[pl.ds(at + r, 1), :] for r in range(rows)], axis=1)
        rank = rank.astype(jnp.float32)
        keys[p : p + 1, :] = rank - items * cluster
        keys[8 + p : 9 + p, :] = rank + items * cluster


def own_kernel(own, sizes, order, unit, best, keys, s, c1, c2):
    n, devices = own.shape[0], lax.axis_size("row")
    make_keys(sizes, order, keys, n, devices, lax.axis_index("row"))
    normalise(own, unit)
    rows = key_rows(keys, 0)
    c1[...], c2[...] = columns(rows[0]), columns(rows[1])
    score(unit, unit, s)
    best[...] = pair_max(s, c1, c2, rows)


def lowest(*outs):
    for out in outs:
        out[...] = jnp.full(out.shape, -1.0, jnp.float32)


def meet(x, y, piece, keys, c1, c2, s, rowbest):
    score(x, y, s)
    return pair_max(s, c1, c2, key_rows(keys, piece), rowbest)


def high_kernel(h, c, d, unit, ownbest, keys, uh, uc, ud, best, cbest, dbest, c1, c2, s, rowbest):
    me = lax.axis_index("row")
    lowest(cbest, dbest)
    best[...] = ownbest[...]

    @pl.when(me > 0)
    def _():
        normalise(h, uh)

    @pl.when(me == 1)
    def _():
        lowest(rowbest)
        own = key_rows(keys, 0)
        c1[...], c2[...] = columns(own[0]), columns(own[1])
        for raw, u, piece, out in ((d, ud, 3, dbest), (c, uc, 1, cbest)):
            normalise(raw, u)
            out[...] = meet(unit, u, piece, keys, c1, c2, s, rowbest)
        best[...] = jnp.maximum(best[...], to_row(rowbest[...]))


def near_kernel(l2, unit, uh, uc, ud, best0, cbest0, dbest0, keys,
                best, hbest, dbest, cross, chip, u2, c1, c2, s, rowbest):
    me = lax.axis_index("row")
    odd = me % 2 == 1
    lowest(hbest, rowbest)
    best[...], dbest[...] = best0[...], dbest0[...]
    cross[...], chip[...] = cbest0[...], cbest0[...]

    @pl.when((me == 1) | (me > 2))
    def _():
        normalise(l2, u2)
        low = key_rows(keys, -1)
        c1[...], c2[...] = columns(low[0]), columns(low[1])

        @pl.when(me == 1)
        def _():
            dbest[...] = jnp.maximum(
                dbest0[...], meet(u2, ud, 3, keys, c1, c2, s, rowbest)
            )
            cross[...] = jnp.maximum(
                cbest0[...], meet(u2, uc, 1, keys, c1, c2, s, rowbest)
            )

        best[...] = jnp.maximum(best0[...], meet(u2, unit, 0, keys, c1, c2, s, rowbest))
        hbest[...] = meet(u2, uh, 2, keys, c1, c2, s, rowbest)
        mine = to_row(rowbest[...])

        @pl.when(odd)
        def _():
            chip[...] = mine

        @pl.when(jnp.logical_not(odd))
        def _():
            cross[...] = mine


def low_kernel(l1, unit, uh, best0, hbest0, dbest0, keys, best, front, rear,
               hbest, l1best, u1, c1, c2, s, rowbest):
    me = lax.axis_index("row")
    best[...], hbest[...] = best0[...], hbest0[...]
    lowest(l1best, rowbest)

    @pl.when(me > 2)
    def _():
        normalise(l1, u1)
        low = key_rows(keys, -2)
        c1[...], c2[...] = columns(low[0]), columns(low[1])
        for y, piece, out in ((unit, 0, best), (uh, 2, hbest)):
            out[...] = jnp.maximum(out[...], meet(u1, y, piece, keys, c1, c2, s, rowbest))
        l1best[...] = to_row(rowbest[...])

    even_chip = (me // 2) % 2 == 0

    @pl.when(even_chip)
    def _():
        front[...] = hbest[...]
        rear[...] = jnp.where(me == 1, dbest0[...], l1best[...])

    @pl.when(jnp.logical_not(even_chip))
    def _():
        front[...] = l1best[...]
        rear[...] = hbest[...]


def call(kernel, outs, scratch, *args):
    return pl.pallas_call(
        kernel,
        out_shape=outs,
        in_specs=[pl.BlockSpec(memory_space=pltpu.VMEM)] * len(args),
        out_specs=[pl.BlockSpec(memory_space=pltpu.VMEM)] * len(outs),
        scratch_shapes=scratch,
        compiler_params=pltpu.CompilerParams(vmem_limit_bytes=16 << 20),
    )(*args)


def completed(some, both, devices):
    used = {i for pair in (*some, *both) for i in pair}
    rest = [i for i in range(devices) if i not in used]
    both = [*both, *zip(rest[::2], rest[1::2])]
    return [*some, *both, *[(j, i) for i, j in both]]


def local(embeddings, sizes, order):
    n, width = embeddings.shape
    devices = lax.axis_size("row")
    sent = (
        [(i, i + 1) for i in range(devices - 1) if i != 1],
        [(4, 1)],
        [(2, 1)],
        [(i, i - 2) for i in range(3, devices)],
        [(i, i + 2) for i in range(1, devices - 2)],
    )
    l2, d, c, h, l1 = [moved(embeddings, pairs) for pairs in sent]

    f32 = functools.partial(jax.ShapeDtypeStruct, dtype=jnp.float32)
    row, unit_ = f32((1, n)), jax.ShapeDtypeStruct((n, width), jnp.bfloat16)
    square, col = pltpu.VMEM((n, n), jnp.float32), pltpu.VMEM((n, LANES), jnp.float32)
    held, line = pltpu.VMEM((n, width), jnp.bfloat16), pltpu.VMEM((1, n), jnp.float32)
    unit, best, keys = call(
        own_kernel, [unit_, row, f32((16, n))], [square, col, col],
        embeddings, sizes.reshape(1, -1), order.reshape(-1, LANES),
    )
    uh, uc, ud, best, cbest, dbest = call(
        high_kernel, [unit_] * 3 + [row] * 3, [col, col, square, col],
        h, c, d, unit, best, keys,
    )
    best, hbest, dbest, cross, chip = call(
        near_kernel, [row] * 5, [held, col, col, square, col],
        l2, unit, uh, uc, ud, best, cbest, dbest, keys,
    )
    best, front, rear = call(
        low_kernel, [row] * 3, [line, line, held, col, col, square, col],
        l1, unit, uh, best, hbest, dbest, keys,
    )
    last = devices - 1
    far = [(i + j, i + j + 2) for i in range(0, devices - 2, 4) for j in range(2)]
    next_ = [(i + j, i + j + 2) for i in range(6, devices - 4, 4) for j in range(2)]
    back = (
        (cross, completed(
            [(1, 2), (2, 0), (0, 1), (last - 1, last - 2), (last - 2, last), (last, last - 1)],
            [(i, i + 1) for i in range(3, last - 2, 2)], devices,
        )),
        (chip, completed([], [(i, i + 1) for i in range(0, devices, 2)], devices)),
        (front, completed([], far, devices)),
        (rear, completed([(1, 4), (4, 2), (2, 0), (0, 1)], [(3, 5), *next_], devices)),
    )
    for (value, pairs) in back:
        best = jnp.maximum(best, moved(value, pairs))
    return best.reshape(n)


def solution(mesh):
    return jax.shard_map(
        local,
        mesh=mesh,
        in_specs=(P(("parts", "row"), None), P("parts"), P("parts")),
        out_specs=P(("parts", "row")),
        check_vma=False,
    )
```

profile of v0, /device:TPU:237, one launch (start us, length us, event | category | flops | bytes accessed | tf_op | source)
XLA Modules:
  0.0 36.1 jit_solution(15526268719524643670)
XLA Ops:
  0.0 1.9 %collective-permute-start.1 = (bf16[512,512]{1,0:T(8,128)(2,1)}, bf16[512,512]{1,0:T(8,128)(2,1)S(1)}, u32[]{:S(2)}, u32[]{:S(2)}) collective-permute-start(bf16[512,512]{1,0:T(8,128)(2,1)} %own.1), channel_id=1, source_target_pairs={{3,1},{4,2},{5,3},{6,4},{7,5},{8,6},{9,7},{10,8},{11,9},{12,10},{1... | collective-permute-start | bytes 1572872 | tf_op jit(solution)/shard_map/ppermute | solution.py:18
  1.9 0.7 %collective-permute-start.2 = (bf16[512,512]{1,0:T(8,128)(2,1)}, bf16[512,512]{1,0:T(8,128)(2,1)S(1)}, u32[]{:S(2)}, u32[]{:S(2)}) collective-permute-start(bf16[512,512]{1,0:T(8,128)(2,1)} %own.1), channel_id=1, source_target_pairs={{2,1},{66,65},{130,129},{194,193}} | collective-permute-start | bytes 1572872 | tf_op jit(solution)/shard_map/ppermute | solution.py:18
  2.6 0.7 %collective-permute-start.3 = (bf16[512,512]{1,0:T(8,128)(2,1)}, bf16[512,512]{1,0:T(8,128)(2,1)S(1)}, u32[]{:S(2)}, u32[]{:S(2)}) collective-permute-start(bf16[512,512]{1,0:T(8,128)(2,1)} %own.1), channel_id=1, source_target_pairs={{4,1},{68,65},{132,129},{196,193}} | collective-permute-start | bytes 1572872 | tf_op jit(solution)/shard_map/ppermute | solution.py:18
  3.4 5.5 %collective-permute-start.4 = (bf16[512,512]{1,0:T(8,128)(2,1)}, bf16[512,512]{1,0:T(8,128)(2,1)S(1)}, u32[]{:S(2)}, u32[]{:S(2)}) collective-permute-start(bf16[512,512]{1,0:T(8,128)(2,1)} %own.1), channel_id=1, source_target_pairs={{0,1},{2,3},{3,4},{4,5},{5,6},{6,7},{7,8},{8,9},{9,10},{10,11},{11... | collective-permute-start | bytes 1572872 | tf_op jit(solution)/shard_map/ppermute | solution.py:18
  8.8 3.8 %collective-permute-start = (bf16[512,512]{1,0:T(8,128)(2,1)}, bf16[512,512]{1,0:T(8,128)(2,1)S(1)}, u32[]{:S(2)}, u32[]{:S(2)}) collective-permute-start(bf16[512,512]{1,0:T(8,128)(2,1)} %own.1), channel_id=1, source_target_pairs={{1,3},{2,4},{3,5},{4,6},{5,7},{6,8},{7,9},{8,10},{9,11},{10,12},{1... | collective-permute-start | bytes 1572872 | tf_op jit(solution)/shard_map/ppermute | solution.py:18
  12.6 0.0 copy-start.2
  12.6 0.6 %copy-done.2 = s32[128]{0:T(128)S(1)} copy-done((s32[128]{0:T(128)S(1)}, s32[128]{0:T(128)}, u32[]{:S(2)}) %copy-start.2) | copy-done | bytes 536
  13.3 0.0 copy-start
  13.3 1.0 %copy-done = bf16[512,512]{1,0:T(8,128)(2,1)S(1)} copy-done((bf16[512,512]{1,0:T(8,128)(2,1)S(1)}, bf16[512,512]{1,0:T(8,128)(2,1)}, u32[]{:S(2)}) %copy-start) | copy-done | bytes 524312
  14.3 0.0 copy-start.1
  14.3 0.9 %copy-done.1 = s32[32768]{0:T(1024)S(1)} copy-done((s32[32768]{0:T(1024)S(1)}, s32[32768]{0:T(1024)}, u32[]{:S(2)}) %copy-start.1) | copy-done | bytes 131096
  15.2 0.8 %shard_map.37 = (bf16[512,512]{1,0:T(8,128)(2,1)S(1)}, f32[1,512]{1,0:T(1,128)S(1)}, f32[16,512]{1,0:T(8,128)S(1)}) custom-call(bf16[512,512]{1,0:T(8,128)(2,1)S(1)} %copy-done, s32[1,128]{1,0:T(1,128)S(1)} %bitcast.4, s32[256,128]{1,0:T(8,128)S(1)} %bitcast.3), custom_call_target="tpu_custom_call" | custom-call | tf_op jit(solution)/shard_map/pallas_call | solution.py:196
  16.1 0.8 %collective-permute-done.1.h = bf16[512,512]{1,0:T(8,128)(2,1)S(1)} collective-permute-done((bf16[512,512]{1,0:T(8,128)(2,1)}, bf16[512,512]{1,0:T(8,128)(2,1)S(1)}, u32[]{:S(2)}, u32[]{:S(2)}) %collective-permute-start.1) | collective-permute-done | bytes 524320 | tf_op jit(solution)/shard_map/ppermute | solution.py:18
  16.9 0.0 collective-permute-done.2.c
  16.9 0.0 collective-permute-done.3.d
  16.9 0.2 shard_map.38
  17.1 1.3 %collective-permute-done.4.l2 = bf16[512,512]{1,0:T(8,128)(2,1)S(1)} collective-permute-done((bf16[512,512]{1,0:T(8,128)(2,1)}, bf16[512,512]{1,0:T(8,128)(2,1)S(1)}, u32[]{:S(2)}, u32[]{:S(2)}) %collective-permute-start.4) | collective-permute-done | bytes 524320 | tf_op jit(solution)/shard_map/ppermute | solution.py:18
  18.3 1.3 %shard_map.39 = (f32[1,512]{1,0:T(1,128)S(1)}, f32[1,512]{1,0:T(1,128)S(1)}, f32[1,512]{1,0:T(1,128)S(1)}, f32[1,512]{1,0:T(1,128)S(1)}, f32[1,512]{1,0:T(1,128)S(1)}) custom-call(bf16[512,512]{1,0:T(8,128)(2,1)S(1)} %collective-permute-done.4.l2, bf16[512,512]{1,0:T(8,128)(2,1)S(1)} %get-tuple-element.22.unit, bf16[512,512]{1,0:T(8,128)(2,1)S(1)} %get-tuple-element.25.uh, ...), custom_call_target="tpu_custom_call" | custom-call | tf_op jit(solution)/shard_map/pallas_call | solution.py:196
  19.7 6.8 %collective-permute-done.l1 = bf16[512,512]{1,0:T(8,128)(2,1)S(1)} collective-permute-done((bf16[512,512]{1,0:T(8,128)(2,1)}, bf16[512,512]{1,0:T(8,128)(2,1)S(1)}, u32[]{:S(2)}, u32[]{:S(2)}) %collective-permute-start) | collective-permute-done | bytes 524320 | tf_op jit(solution)/shard_map/ppermute | solution.py:18
  26.5 1.0 %shard_map.40 = (f32[1,512]{1,0:T(1,128)S(1)}, f32[1,512]{1,0:T(1,128)S(1)}, f32[1,512]{1,0:T(1,128)S(1)}) custom-call(bf16[512,512]{1,0:T(8,128)(2,1)S(1)} %collective-permute-done.l1, bf16[512,512]{1,0:T(8,128)(2,1)S(1)} %get-tuple-element.22.unit, bf16[512,512]{1,0:T(8,128)(2,1)S(1)} %get-tuple-element.25.uh, f32[1,512]{1,0:T(1,128)S(1)} %get-tuple-element.31.best0, ...), custom_call_target="tpu_custom_call" | custom-call | tf_op jit(solution)/shard_map/pallas_call | solution.py:196
  27.5 0.1 collective-permute-start.7
  27.7 3.7 %collective-permute-start.8 = (f32[1,512]{1,0:T(1,128)S(1)}, f32[1,512]{1,0:T(1,128)S(1)}, u32[]{:S(2)}, u32[]{:S(2)}) collective-permute-start(f32[1,512]{1,0:T(1,128)S(1)} %get-tuple-element.38), channel_id=1, source_target_pairs={{1,4},{4,2},{2,0},{0,1},{3,5},{6,8},{7,9},{10,12},{11,13},{14,16},... | collective-permute-start | bytes 6152 | tf_op jit(solution)/shard_map/ppermute | solution.py:18
  31.3 0.0 collective-permute-start.5
  31.3 0.0 collective-permute-start.6
  31.3 0.0 collective-permute-done.7
  31.3 1.0 %collective-permute-done.8 = f32[1,512]{1,0:T(1,128)S(1)} collective-permute-done((f32[1,512]{1,0:T(1,128)S(1)}, f32[1,512]{1,0:T(1,128)S(1)}, u32[]{:S(2)}, u32[]{:S(2)}) %collective-permute-start.8) | collective-permute-done | bytes 2080 | tf_op jit(solution)/shard_map/ppermute | solution.py:18
  32.3 3.2 %collective-permute-done.5 = f32[1,512]{1,0:T(1,128)S(1)} collective-permute-done((f32[1,512]{1,0:T(1,128)S(1)}, f32[1,512]{1,0:T(1,128)S(1)}, u32[]{:S(2)}, u32[]{:S(2)}) %collective-permute-start.5) | collective-permute-done | bytes 2080 | tf_op jit(solution)/shard_map/ppermute | solution.py:18
  35.5 0.0 collective-permute-done.6
  35.5 0.6 %maximum_maximum_fusion = f32[1,512]{1,0:T(1,128)} fusion(f32[1,512]{1,0:T(1,128)S(1)} %collective-permute-done.8, f32[1,512]{1,0:T(1,128)S(1)} %collective-permute-done.7, f32[1,512]{1,0:T(1,128)S(1)} %collective-permute-done.6, f32[1,512]{1,0:T(1,128)S(1)} %get-tuple-element.34, f32[1,512]{1,0:T(1,128)S(1)} %collective-permute-done.5), kind=kLoop, calls=%fused_computation | loop fusion | flops 2048 | bytes 12288 | tf_op jit(solution)/shard_map/max | solution.py:258
Async XLA Ops:
  0.0 16.9 %collective-permute-start.1 = (bf16[512,512]{1,0:T(8,128)(2,1)}, bf16[512,512]{1,0:T(8,128)(2,1)S(1)}, u32[]{:S(2)}, u32[]{:S(2)}) collective-permute-start(bf16[512,512]{1,0:T(8,128)(2,1)} %own.1), channel_id=1, source_target_pairs={{3,1},{4,2},{5,3},{6,4},{7,5},{8,6},{9,7},{10,8},{11,9},{12,10},{1... | collective-permute-start | bytes 1572872 | tf_op jit(solution)/shard_map/ppermute | solution.py:18
  1.9 14.9 %collective-permute-start.2 = (bf16[512,512]{1,0:T(8,128)(2,1)}, bf16[512,512]{1,0:T(8,128)(2,1)S(1)}, u32[]{:S(2)}, u32[]{:S(2)}) collective-permute-start(bf16[512,512]{1,0:T(8,128)(2,1)} %own.1), channel_id=1, source_target_pairs={{2,1},{66,65},{130,129},{194,193}} | collective-permute-start | bytes 1572872 | tf_op jit(solution)/shard_map/ppermute | solution.py:18
  2.6 14.2 %collective-permute-start.3 = (bf16[512,512]{1,0:T(8,128)(2,1)}, bf16[512,512]{1,0:T(8,128)(2,1)S(1)}, u32[]{:S(2)}, u32[]{:S(2)}) collective-permute-start(bf16[512,512]{1,0:T(8,128)(2,1)} %own.1), channel_id=1, source_target_pairs={{4,1},{68,65},{132,129},{196,193}} | collective-permute-start | bytes 1572872 | tf_op jit(solution)/shard_map/ppermute | solution.py:18
  3.4 15.0 %collective-permute-start.4 = (bf16[512,512]{1,0:T(8,128)(2,1)}, bf16[512,512]{1,0:T(8,128)(2,1)S(1)}, u32[]{:S(2)}, u32[]{:S(2)}) collective-permute-start(bf16[512,512]{1,0:T(8,128)(2,1)} %own.1), channel_id=1, source_target_pairs={{0,1},{2,3},{3,4},{4,5},{5,6},{6,7},{7,8},{8,9},{9,10},{10,11},{11... | collective-permute-start | bytes 1572872 | tf_op jit(solution)/shard_map/ppermute | solution.py:18
  8.8 17.7 %collective-permute-start = (bf16[512,512]{1,0:T(8,128)(2,1)}, bf16[512,512]{1,0:T(8,128)(2,1)S(1)}, u32[]{:S(2)}, u32[]{:S(2)}) collective-permute-start(bf16[512,512]{1,0:T(8,128)(2,1)} %own.1), channel_id=1, source_target_pairs={{1,3},{2,4},{3,5},{4,6},{5,7},{6,8},{7,9},{8,10},{9,11},{10,12},{1... | collective-permute-start | bytes 1572872 | tf_op jit(solution)/shard_map/ppermute | solution.py:18
  12.6 0.7 %copy-start.2 = (s32[128]{0:T(128)S(1)}, s32[128]{0:T(128)}, u32[]{:S(2)}) copy-start(s32[128]{0:T(128)} %param.4) | copy-start | bytes 1540
  13.3 1.0 %copy-start = (bf16[512,512]{1,0:T(8,128)(2,1)S(1)}, bf16[512,512]{1,0:T(8,128)(2,1)}, u32[]{:S(2)}) copy-start(bf16[512,512]{1,0:T(8,128)(2,1)} %own.1) | copy-start | bytes 1572868
  14.3 0.9 %copy-start.1 = (s32[32768]{0:T(1024)S(1)}, s32[32768]{0:T(1024)}, u32[]{:S(2)}) copy-start(s32[32768]{0:T(1024)} %param.5) | copy-start | bytes 393220
  27.5 3.8 %collective-permute-start.7 = (f32[1,512]{1,0:T(1,128)S(1)}, f32[1,512]{1,0:T(1,128)S(1)}, u32[]{:S(2)}, u32[]{:S(2)}) collective-permute-start(f32[1,512]{1,0:T(1,128)S(1)} %get-tuple-element.37), channel_id=1, source_target_pairs={{0,2},{1,3},{4,6},{5,7},{8,10},{9,11},{12,14},{13,15},{16,18},{17,... | collective-permute-start | bytes 6152 | tf_op jit(solution)/shard_map/ppermute | solution.py:18
  27.7 4.6 %collective-permute-start.8 = (f32[1,512]{1,0:T(1,128)S(1)}, f32[1,512]{1,0:T(1,128)S(1)}, u32[]{:S(2)}, u32[]{:S(2)}) collective-permute-start(f32[1,512]{1,0:T(1,128)S(1)} %get-tuple-element.38), channel_id=1, source_target_pairs={{1,4},{4,2},{2,0},{0,1},{3,5},{6,8},{7,9},{10,12},{11,13},{14,16},... | collective-permute-start | bytes 6152 | tf_op jit(solution)/shard_map/ppermute | solution.py:18
  31.3 4.2 %collective-permute-start.5 = (f32[1,512]{1,0:T(1,128)S(1)}, f32[1,512]{1,0:T(1,128)S(1)}, u32[]{:S(2)}, u32[]{:S(2)}) collective-permute-start(f32[1,512]{1,0:T(1,128)S(1)} %get-tuple-element.35), channel_id=1, source_target_pairs={{1,2},{2,0},{0,1},{62,61},{61,63},{63,62},{3,4},{5,6},{7,8},{9,10}... | collective-permute-start | bytes 6152 | tf_op jit(solution)/shard_map/ppermute | solution.py:18
  31.3 4.2 %collective-permute-start.6 = (f32[1,512]{1,0:T(1,128)S(1)}, f32[1,512]{1,0:T(1,128)S(1)}, u32[]{:S(2)}, u32[]{:S(2)}) collective-permute-start(f32[1,512]{1,0:T(1,128)S(1)} %get-tuple-element.36), channel_id=1, source_target_pairs={{0,1},{2,3},{4,5},{6,7},{8,9},{10,11},{12,13},{14,15},{16,17},{18,... | collective-permute-start | bytes 6152 | tf_op jit(solution)/shard_map/ppermute | solution.py:18
where the time goes:
time: 36.4 us; the launch traced here: 36.1 us
  starting transfers between devices  16.4 us (45%)
  waiting for transfers between devices  13.1 us (36%)
  Pallas kernels  3.33 us (9%)
  local copies, waits for them, and re-layouts  2.59 us (7%)
  other arithmetic  0.59 us (2%)
    ppermute x9, starting transfers between devices, moved(): return lax.ppermute(x, 'row', pairs)  16.4 us
    ppermute x9, waiting for transfers between devices, moved(): return lax.ppermute(x, 'row', pairs)  13.1 us
    pallas_call x4, Pallas kernels, call(): pl.pallas_call(kernel, out_shape=outs, in_specs=[pl.BlockSpec(memory_spac...  3.33 us
    unnamed x6, local copies, waits for them, and re-layouts  2.59 us
  transfers between devices with their start and end apart: 9, of which 5 were waited for; matrix products, arithmetic and copies ran while one was open for 0% of the time, Pallas kernels for 6%

commit v1 on v0

--- a/solution.py
+++ b/solution.py
@@ -88,7 +88,15 @@
         keys[8 + p : 9 + p, :] = rank + items * cluster
 
 
-def own_kernel(own, sizes, order, unit, best, keys, s, c1, c2):
+def own_kernel(own_, sizes_, order_, unit, best, keys, s, c1, c2, own, sizes, order, sem):
+    copies = [
+        pltpu.make_async_copy(src, dst, sem.at[i])
+        for i, (src, dst) in enumerate(((sizes_, sizes), (order_, order), (own_, own)))
+    ]
+    for copy in copies:
+        copy.start()
+    for copy in copies:
+        copy.wait()
     n, devices = own.shape[0], lax.axis_size("row")
     make_keys(sizes, order, keys, n, devices, lax.axis_index("row"))
     normalise(own, unit)
@@ -108,33 +116,24 @@
     return pair_max(s, c1, c2, key_rows(keys, piece), rowbest)
 
 
-def high_kernel(h, c, d, unit, ownbest, keys, uh, uc, ud, best, cbest, dbest, c1, c2, s, rowbest):
-    me = lax.axis_index("row")
-    lowest(cbest, dbest)
-    best[...] = ownbest[...]
-
-    @pl.when(me > 0)
-    def _():
-        normalise(h, uh)
-
-    @pl.when(me == 1)
+def edge_kernel(c, unit, best0, keys, uc, best, cbest, c1, c2, s, rowbest):
+    lowest(cbest)
+    best[...] = best0[...]
+
+    @pl.when(lax.axis_index("row") == 1)
     def _():
         lowest(rowbest)
         own = key_rows(keys, 0)
         c1[...], c2[...] = columns(own[0]), columns(own[1])
-        for raw, u, piece, out in ((d, ud, 3, dbest), (c, uc, 1, cbest)):
-            normalise(raw, u)
-            out[...] = meet(unit, u, piece, keys, c1, c2, s, rowbest)
+        normalise(c, uc)
+        cbest[...] = meet(unit, uc, 1, keys, c1, c2, s, rowbest)
         best[...] = jnp.maximum(best[...], to_row(rowbest[...]))
 
 
-def near_kernel(l2, unit, uh, uc, ud, best0, cbest0, dbest0, keys,
-                best, hbest, dbest, cross, chip, u2, c1, c2, s, rowbest):
+def near_kernel(l2, unit, uc, best0, cbest0, keys, best, cbest, u2, c1, c2, rowbest, s):
     me = lax.axis_index("row")
-    odd = me % 2 == 1
-    lowest(hbest, rowbest)
-    best[...], dbest[...] = best0[...], dbest0[...]
-    cross[...], chip[...] = cbest0[...], cbest0[...]
+    lowest(rowbest)
+    best[...], cbest[...] = best0[...], cbest0[...]
 
     @pl.when((me == 1) | (me > 2))
     def _():
@@ -142,37 +141,58 @@
         low = key_rows(keys, -1)
         c1[...], c2[...] = columns(low[0]), columns(low[1])
 
+        def add(y, piece, out):
+            out[...] = jnp.maximum(out[...], meet(u2, y, piece, keys, c1, c2, s, rowbest))
+
         @pl.when(me == 1)
         def _():
-            dbest[...] = jnp.maximum(
-                dbest0[...], meet(u2, ud, 3, keys, c1, c2, s, rowbest)
-            )
-            cross[...] = jnp.maximum(
-                cbest0[...], meet(u2, uc, 1, keys, c1, c2, s, rowbest)
-            )
-
-        best[...] = jnp.maximum(best0[...], meet(u2, unit, 0, keys, c1, c2, s, rowbest))
+            add(uc, 1, cbest)
+
+        add(unit, 0, best)
+
+
+def high_kernel(h, u2, c1, c2, rowbest0, keys, uh, hbest, l2best, rowbest, s):
+    lowest(hbest, l2best)
+    rowbest[...] = rowbest0[...]
+    me = lax.axis_index("row")
+
+    @pl.when((me == 1) | (me > 2))
+    def _():
+        normalise(h, uh)
         hbest[...] = meet(u2, uh, 2, keys, c1, c2, s, rowbest)
-        mine = to_row(rowbest[...])
-
-        @pl.when(odd)
-        def _():
-            chip[...] = mine
-
-        @pl.when(jnp.logical_not(odd))
-        def _():
-            cross[...] = mine
-
-
-def low_kernel(l1, unit, uh, best0, hbest0, dbest0, keys, best, front, rear,
-               hbest, l1best, u1, c1, c2, s, rowbest):
+        l2best[...] = to_row(rowbest[...])
+
+
+def low_kernel(l1, edge, unit, uh, u2, e1, e2, rowbest0, best0, hbest0, l2best, cbest, keys,
+               best, front, rear, cross, chip, hbest, l1best, u1, c1, c2, s, rowbest, nearbest):
     me = lax.axis_index("row")
+    odd = me % 2 == 1
     best[...], hbest[...] = best0[...], hbest0[...]
     lowest(l1best, rowbest)
+    chip[...] = jnp.where(odd, l2best[...], -1.0)
+    cross[...] = jnp.where(odd, cbest[...], l2best[...])
+
+    @pl.when(me == 1)
+    def _():
+        normalise(l1, u1)
+        own = key_rows(keys, 0)
+        c1[...], c2[...] = columns(own[0]), columns(own[1])
+        first = meet(unit, u1, 3, keys, c1, c2, s, rowbest)
+        best[...] = jnp.maximum(best[...], to_row(rowbest[...]))
+        nearbest[...] = rowbest0[...]
+        l1best[...] = jnp.maximum(first, meet(u2, u1, 3, keys, e1, e2, s, nearbest))
+        chip[...] = to_row(nearbest[...])
 
     @pl.when(me > 2)
     def _():
-        normalise(l1, u1)
+        @pl.when(me == 6)
+        def _():
+            normalise(edge, u1)
+
+        @pl.when(me != 6)
+        def _():
+            normalise(l1, u1)
+
         low = key_rows(keys, -2)
         c1[...], c2[...] = columns(low[0]), columns(low[1])
         for y, piece, out in ((unit, 0, best), (uh, 2, hbest)):
@@ -184,7 +204,7 @@
     @pl.when(even_chip)
     def _():
         front[...] = hbest[...]
-        rear[...] = jnp.where(me == 1, dbest0[...], l1best[...])
+        rear[...] = l1best[...]
 
     @pl.when(jnp.logical_not(even_chip))
     def _():
@@ -192,11 +212,11 @@
         rear[...] = hbest[...]
 
 
-def call(kernel, outs, scratch, *args):
+def call(kernel, outs, scratch, *args, space=pltpu.VMEM):
     return pl.pallas_call(
         kernel,
         out_shape=outs,
-        in_specs=[pl.BlockSpec(memory_space=pltpu.VMEM)] * len(args),
+        in_specs=[pl.BlockSpec(memory_space=space)] * len(args),
         out_specs=[pl.BlockSpec(memory_space=pltpu.VMEM)] * len(outs),
         scratch_shapes=scratch,
         compiler_params=pltpu.CompilerParams(vmem_limit_bytes=16 << 20),
@@ -215,32 +235,38 @@
     devices = lax.axis_size("row")
     sent = (
         [(i, i + 1) for i in range(devices - 1) if i != 1],
-        [(4, 1)],
-        [(2, 1)],
-        [(i, i - 2) for i in range(3, devices)],
-        [(i, i + 2) for i in range(1, devices - 2)],
-    )
-    l2, d, c, h, l1 = [moved(embeddings, pairs) for pairs in sent]
+        [(i, i - 2) for i in range(3, devices) if i != 4],
+        [(2, 1), (4, 6)],
+        [(i, 1 if i == 4 else i + 2) for i in range(1, devices - 2)],
+    )
+    l2, h, edge, l1 = [moved(embeddings, pairs) for pairs in sent]
 
     f32 = functools.partial(jax.ShapeDtypeStruct, dtype=jnp.float32)
     row, unit_ = f32((1, n)), jax.ShapeDtypeStruct((n, width), jnp.bfloat16)
     square, col = pltpu.VMEM((n, n), jnp.float32), pltpu.VMEM((n, LANES), jnp.float32)
     held, line = pltpu.VMEM((n, width), jnp.bfloat16), pltpu.VMEM((1, n), jnp.float32)
+    in_hbm = functools.partial(pltpu.with_memory_space_constraint, memory_space=pltpu.HBM)
+    sizes, order = sizes.reshape(1, -1), order.reshape(-1, LANES)
     unit, best, keys = call(
-        own_kernel, [unit_, row, f32((16, n))], [square, col, col],
-        embeddings, sizes.reshape(1, -1), order.reshape(-1, LANES),
-    )
-    uh, uc, ud, best, cbest, dbest = call(
-        high_kernel, [unit_] * 3 + [row] * 3, [col, col, square, col],
-        h, c, d, unit, best, keys,
-    )
-    best, hbest, dbest, cross, chip = call(
-        near_kernel, [row] * 5, [held, col, col, square, col],
-        l2, unit, uh, uc, ud, best, cbest, dbest, keys,
-    )
-    best, front, rear = call(
-        low_kernel, [row] * 3, [line, line, held, col, col, square, col],
-        l1, unit, uh, best, hbest, dbest, keys,
+        own_kernel,
+        [unit_, row, f32((16, n))],
+        [square, col, col, held, pltpu.VMEM(sizes.shape, jnp.int32),
+         pltpu.VMEM(order.shape, jnp.int32), pltpu.SemaphoreType.DMA((3,))],
+        *[in_hbm(x) for x in (embeddings, sizes, order)], space=pltpu.HBM,
+    )
+    uc, best, cbest = call(
+        edge_kernel, [unit_] + [row] * 2, [col, col, square, col], edge, unit, best, keys
+    )
+    wide = f32((n, LANES))
+    best, cbest, u2, c1, c2, rowbest = call(
+        near_kernel, [row] * 2 + [unit_] + [wide] * 3, [square], l2, unit, uc, best, cbest, keys
+    )
+    uh, hbest, l2best, rowbest = call(
+        high_kernel, [unit_, row, row, wide], [square], h, u2, c1, c2, rowbest, keys
+    )
+    best, front, rear, cross, chip = call(
+        low_kernel, [row] * 5, [line, line, held, col, col, square, col, col],
+        l1, edge, unit, uh, u2, c1, c2, rowbest, best, hbest, l2best, cbest, keys,
     )
     last = devices - 1
     far = [(i + j, i + j + 2) for i in range(0, devices - 2, 4) for j in range(2)]
@@ -250,9 +276,9 @@
             [(1, 2), (2, 0), (0, 1), (last - 1, last - 2), (last - 2, last), (last, last - 1)],
             [(i, i + 1) for i in range(3, last - 2, 2)], devices,
         )),
+        (rear, completed([(1, 4), (4, 2), (2, 0), (0, 1)], [(3, 5), *next_], devices)),
+        (front, completed([], far, devices)),
         (chip, completed([], [(i, i + 1) for i in range(0, devices, 2)], devices)),
-        (front, completed([], far, devices)),
-        (rear, completed([(1, 4), (4, 2), (2, 0), (0, 1)], [(3, 5), *next_], devices)),
     )
     for (value, pairs) in back:
         best = jnp.maximum(best, moved(value, pairs))

time: 36.4 us -> 34.7 us (0.953)
  the two profiles are of different devices: /device:TPU:237 before, /device:TPU:37 now
where the time goes in v1:
time: 34.7 us; the launch traced here: 34.5 us
  starting transfers between devices  19.1 us (55%)
  waiting for transfers between devices  8.65 us (25%)
  Pallas kernels  6.04 us (17%)
  other arithmetic  0.59 us (2%)
    ppermute x8, starting transfers between devices, moved(): return lax.ppermute(x, 'row', pairs)  19.1 us
    ppermute x8, waiting for transfers between devices, moved(): return lax.ppermute(x, 'row', pairs)  8.65 us
    pallas_call x5, Pallas kernels, call(): pl.pallas_call(kernel, out_shape=outs, in_specs=[pl.BlockSpec(memory_spac...  6.04 us
  transfers between devices with their start and end apart: 8, of which 4 were waited for; matrix products, arithmetic and copies ran while one was open for 0% of the time, Pallas kernels for 14%

profile of v1, /device:TPU:37, one launch (start us, length us, event | category | flops | bytes accessed | tf_op | source)
XLA Modules:
  0.0 34.5 jit_solution(4284198759666970150)
XLA Ops:
  0.0 1.3 %collective-permute-start.1 = (bf16[512,512]{1,0:T(8,128)(2,1)}, bf16[512,512]{1,0:T(8,128)(2,1)S(1)}, u32[]{:S(2)}, u32[]{:S(2)}) collective-permute-start(bf16[512,512]{1,0:T(8,128)(2,1)} %own_.1), channel_id=1, source_target_pairs={{2,1},{4,6},{66,65},{68,70},{130,129},{132,134},{194,193},{196,198}} | collective-permute-start | bytes 1572872 | tf_op jit(solution)/shard_map/ppermute | solution.py:18
  1.3 1.3 %collective-permute-start.3 = (bf16[512,512]{1,0:T(8,128)(2,1)}, bf16[512,512]{1,0:T(8,128)(2,1)S(1)}, u32[]{:S(2)}, u32[]{:S(2)}) collective-permute-start(bf16[512,512]{1,0:T(8,128)(2,1)} %own_.1), channel_id=1, source_target_pairs={{0,1},{2,3},{3,4},{4,5},{5,6},{6,7},{7,8},{8,9},{9,10},{10,11},{11... | collective-permute-start | bytes 1572872 | tf_op jit(solution)/shard_map/ppermute | solution.py:18
  2.6 1.3 %collective-permute-start.2 = (bf16[512,512]{1,0:T(8,128)(2,1)}, bf16[512,512]{1,0:T(8,128)(2,1)S(1)}, u32[]{:S(2)}, u32[]{:S(2)}) collective-permute-start(bf16[512,512]{1,0:T(8,128)(2,1)} %own_.1), channel_id=1, source_target_pairs={{3,1},{5,3},{6,4},{7,5},{8,6},{9,7},{10,8},{11,9},{12,10},{13,11},... | collective-permute-start | bytes 1572872 | tf_op jit(solution)/shard_map/ppermute | solution.py:18
  3.9 11.0 %collective-permute-start = (bf16[512,512]{1,0:T(8,128)(2,1)}, bf16[512,512]{1,0:T(8,128)(2,1)S(1)}, u32[]{:S(2)}, u32[]{:S(2)}) collective-permute-start(bf16[512,512]{1,0:T(8,128)(2,1)} %own_.1), channel_id=1, source_target_pairs={{1,3},{2,4},{3,5},{4,1},{5,7},{6,8},{7,9},{8,10},{9,11},{10,12},{1... | collective-permute-start | bytes 1572872 | tf_op jit(solution)/shard_map/ppermute | solution.py:18
  14.9 2.0 %shard_map.37 = (bf16[512,512]{1,0:T(8,128)(2,1)S(1)}, f32[1,512]{1,0:T(1,128)S(1)}, f32[16,512]{1,0:T(8,128)S(1)}) custom-call(bf16[512,512]{1,0:T(8,128)(2,1)} %own_.1, s32[1,128]{1,0:T(1,128)} %bitcast.4, s32[256,128]{1,0:T(8,128)} %bitcast.3), custom_call_target="tpu_custom_call" | custom-call | tf_op jit(solution)/shard_map/pallas_call | solution.py:216
  16.9 0.0 collective-permute-done.1.c.edge
  16.9 0.8 %shard_map.38 = (bf16[512,512]{1,0:T(8,128)(2,1)S(1)}, f32[1,512]{1,0:T(1,128)S(1)}, f32[1,512]{1,0:T(1,128)S(1)}) custom-call(bf16[512,512]{1,0:T(8,128)(2,1)S(1)} %collective-permute-done.1.c.edge, bf16[512,512]{1,0:T(8,128)(2,1)S(1)} %get-tuple-element.26.unit, f32[1,512]{1,0:T(1,128)S(1)} %get-tuple-element.27.best0, f32[16,512]{1,0:T(8,128)S(1)} %get-tuple-element.28.keys), custom_call_target="tpu_custom_call" | custom-call | tf_op jit(solution)/shard_map/pallas_call | solution.py:216
  17.7 6.4 %collective-permute-done.3.l2 = bf16[512,512]{1,0:T(8,128)(2,1)S(1)} collective-permute-done((bf16[512,512]{1,0:T(8,128)(2,1)}, bf16[512,512]{1,0:T(8,128)(2,1)S(1)}, u32[]{:S(2)}, u32[]{:S(2)}) %collective-permute-start.3) | collective-permute-done | bytes 524320 | tf_op jit(solution)/shard_map/ppermute | solution.py:18
  24.0 1.4 %shard_map.39 = (f32[1,512]{1,0:T(1,128)S(1)}, f32[1,512]{1,0:T(1,128)S(1)}, bf16[512,512]{1,0:T(8,128)(2,1)S(1)}, f32[512,128]{1,0:T(8,128)S(1)}, f32[512,128]{1,0:T(8,128)S(1)}, /*index=5*/f32[512,128]{1,0:T(8,128)S(1)}) custom-call(bf16[512,512]{1,0:T(8,128)(2,1)S(1)} %collective-permute-done.3.l2, bf16[512,512]{1,0:T(8,128)(2,1)S(1)} %get-tuple-element.26.unit, ...), custom_call_target="tpu_custom_call" | custom-call | tf_op jit(solution)/shard_map/pallas_call | solution.py:216
  25.4 0.0 collective-permute-done.2.h
  25.5 0.8 %shard_map.40 = (bf16[512,512]{1,0:T(8,128)(2,1)S(1)}, f32[1,512]{1,0:T(1,128)S(1)}, f32[1,512]{1,0:T(1,128)S(1)}, f32[512,128]{1,0:T(8,128)S(1)}) custom-call(bf16[512,512]{1,0:T(8,128)(2,1)S(1)} %collective-permute-done.2.h, bf16[512,512]{1,0:T(8,128)(2,1)S(1)} %get-tuple-element.32.u2, f32[512,128]{1,0:T(8,128)S(1)} %get-tuple-element.33.c1.e1, ...), custom_call_target="tpu_custom_call" | custom-call | tf_op jit(solution)/shard_map/pallas_call | solution.py:216
  26.2 0.3 collective-permute-done.l1
  26.5 1.1 %shard_map.41 = (f32[1,512]{1,0:T(1,128)S(1)}, f32[1,512]{1,0:T(1,128)S(1)}, f32[1,512]{1,0:T(1,128)S(1)}, f32[1,512]{1,0:T(1,128)S(1)}, f32[1,512]{1,0:T(1,128)S(1)}) custom-call(bf16[512,512]{1,0:T(8,128)(2,1)S(1)} %collective-permute-done.l1, bf16[512,512]{1,0:T(8,128)(2,1)S(1)} %collective-permute-done.1.c.edge, ...), custom_call_target="tpu_custom_call" | custom-call | tf_op jit(solution)/shard_map/pallas_call | solution.py:216
  27.7 0.2 collective-permute-start.4
  27.8 3.6 %collective-permute-start.5 = (f32[1,512]{1,0:T(1,128)S(1)}, f32[1,512]{1,0:T(1,128)S(1)}, u32[]{:S(2)}, u32[]{:S(2)}) collective-permute-start(f32[1,512]{1,0:T(1,128)S(1)} %get-tuple-element.44), channel_id=1, source_target_pairs={{1,4},{4,2},{2,0},{0,1},{3,5},{6,8},{7,9},{10,12},{11,13},{14,16},... | collective-permute-start | bytes 6152 | tf_op jit(solution)/shard_map/ppermute | solution.py:18
  31.5 0.4 %collective-permute-start.6 = (f32[1,512]{1,0:T(1,128)S(1)}, f32[1,512]{1,0:T(1,128)S(1)}, u32[]{:S(2)}, u32[]{:S(2)}) collective-permute-start(f32[1,512]{1,0:T(1,128)S(1)} %get-tuple-element.45), channel_id=1, source_target_pairs={{0,2},{1,3},{4,6},{5,7},{8,10},{9,11},{12,14},{13,15},{16,18},{17,... | collective-permute-start | bytes 6152 | tf_op jit(solution)/shard_map/ppermute | solution.py:18
  31.9 0.0 collective-permute-start.7
  31.9 0.0 collective-permute-done.4
  31.9 0.3 collective-permute-done.5
  32.2 1.7 %collective-permute-done.6 = f32[1,512]{1,0:T(1,128)S(1)} collective-permute-done((f32[1,512]{1,0:T(1,128)S(1)}, f32[1,512]{1,0:T(1,128)S(1)}, u32[]{:S(2)}, u32[]{:S(2)}) %collective-permute-start.6) | collective-permute-done | bytes 2080 | tf_op jit(solution)/shard_map/ppermute | solution.py:18
  33.9 0.0 collective-permute-done.7
  33.9 0.6 %maximum_maximum_fusion = f32[1,512]{1,0:T(1,128)} fusion(f32[1,512]{1,0:T(1,128)S(1)} %collective-permute-done.7, f32[1,512]{1,0:T(1,128)S(1)} %collective-permute-done.6, f32[1,512]{1,0:T(1,128)S(1)} %collective-permute-done.5, f32[1,512]{1,0:T(1,128)S(1)} %get-tuple-element.42, f32[1,512]{1,0:T(1,128)S(1)} %collective-permute-done.4), kind=kLoop, calls=%fused_computation | loop fusion | flops 2048 | bytes 12288 | tf_op jit(solution)/shard_map/max | solution.py:284
Async XLA Ops:
  0.0 16.9 %collective-permute-start.1 = (bf16[512,512]{1,0:T(8,128)(2,1)}, bf16[512,512]{1,0:T(8,128)(2,1)S(1)}, u32[]{:S(2)}, u32[]{:S(2)}) collective-permute-start(bf16[512,512]{1,0:T(8,128)(2,1)} %own_.1), channel_id=1, source_target_pairs={{2,1},{4,6},{66,65},{68,70},{130,129},{132,134},{194,193},{196,198}} | collective-permute-start | bytes 1572872 | tf_op jit(solution)/shard_map/ppermute | solution.py:18
  1.3 22.7 %collective-permute-start.3 = (bf16[512,512]{1,0:T(8,128)(2,1)}, bf16[512,512]{1,0:T(8,128)(2,1)S(1)}, u32[]{:S(2)}, u32[]{:S(2)}) collective-permute-start(bf16[512,512]{1,0:T(8,128)(2,1)} %own_.1), channel_id=1, source_target_pairs={{0,1},{2,3},{3,4},{4,5},{5,6},{6,7},{7,8},{8,9},{9,10},{10,11},{11... | collective-permute-start | bytes 1572872 | tf_op jit(solution)/shard_map/ppermute | solution.py:18
  2.6 22.8 %collective-permute-start.2 = (bf16[512,512]{1,0:T(8,128)(2,1)}, bf16[512,512]{1,0:T(8,128)(2,1)S(1)}, u32[]{:S(2)}, u32[]{:S(2)}) collective-permute-start(bf16[512,512]{1,0:T(8,128)(2,1)} %own_.1), channel_id=1, source_target_pairs={{3,1},{5,3},{6,4},{7,5},{8,6},{9,7},{10,8},{11,9},{12,10},{13,11},... | collective-permute-start | bytes 1572872 | tf_op jit(solution)/shard_map/ppermute | solution.py:18
  3.9 22.6 %collective-permute-start = (bf16[512,512]{1,0:T(8,128)(2,1)}, bf16[512,512]{1,0:T(8,128)(2,1)S(1)}, u32[]{:S(2)}, u32[]{:S(2)}) collective-permute-start(bf16[512,512]{1,0:T(8,128)(2,1)} %own_.1), channel_id=1, source_target_pairs={{1,3},{2,4},{3,5},{4,1},{5,7},{6,8},{7,9},{8,10},{9,11},{10,12},{1... | collective-permute-start | bytes 1572872 | tf_op jit(solution)/shard_map/ppermute | solution.py:18
  27.7 4.3 %collective-permute-start.4 = (f32[1,512]{1,0:T(1,128)S(1)}, f32[1,512]{1,0:T(1,128)S(1)}, u32[]{:S(2)}, u32[]{:S(2)}) collective-permute-start(f32[1,512]{1,0:T(1,128)S(1)} %get-tuple-element.43), channel_id=1, source_target_pairs={{1,2},{2,0},{0,1},{62,61},{61,63},{63,62},{3,4},{5,6},{7,8},{9,10}... | collective-permute-start | bytes 6152 | tf_op jit(solution)/shard_map/ppermute | solution.py:18
  27.8 4.4 %collective-permute-start.5 = (f32[1,512]{1,0:T(1,128)S(1)}, f32[1,512]{1,0:T(1,128)S(1)}, u32[]{:S(2)}, u32[]{:S(2)}) collective-permute-start(f32[1,512]{1,0:T(1,128)S(1)} %get-tuple-element.44), channel_id=1, source_target_pairs={{1,4},{4,2},{2,0},{0,1},{3,5},{6,8},{7,9},{10,12},{11,13},{14,16},... | collective-permute-start | bytes 6152 | tf_op jit(solution)/shard_map/ppermute | solution.py:18
  31.5 2.4 %collective-permute-start.6 = (f32[1,512]{1,0:T(1,128)S(1)}, f32[1,512]{1,0:T(1,128)S(1)}, u32[]{:S(2)}, u32[]{:S(2)}) collective-permute-start(f32[1,512]{1,0:T(1,128)S(1)} %get-tuple-element.45), channel_id=1, source_target_pairs={{0,2},{1,3},{4,6},{5,7},{8,10},{9,11},{12,14},{13,15},{16,18},{17,... | collective-permute-start | bytes 6152 | tf_op jit(solution)/shard_map/ppermute | solution.py:18
  31.9 2.0 %collective-permute-start.7 = (f32[1,512]{1,0:T(1,128)S(1)}, f32[1,512]{1,0:T(1,128)S(1)}, u32[]{:S(2)}, u32[]{:S(2)}) collective-permute-start(f32[1,512]{1,0:T(1,128)S(1)} %get-tuple-element.46), channel_id=1, source_target_pairs={{0,1},{2,3},{4,5},{6,7},{8,9},{10,11},{12,13},{14,15},{16,17},{18,... | collective-permute-start | bytes 6152 | tf_op jit(solution)/shard_map/ppermute | solution.py:18

commit v2 on v1

--- a/solution.py
+++ b/solution.py
@@ -151,7 +151,7 @@
         add(unit, 0, best)
 
 
-def high_kernel(h, u2, c1, c2, rowbest0, keys, uh, hbest, l2best, rowbest, s):
+def high_kernel(h, u2, c1, c2, rowbest0, keys, uh, hbest, l2best, rowbest, d1, d2, s):
     lowest(hbest, l2best)
     rowbest[...] = rowbest0[...]
     me = lax.axis_index("row")
@@ -161,10 +161,13 @@
         normalise(h, uh)
         hbest[...] = meet(u2, uh, 2, keys, c1, c2, s, rowbest)
         l2best[...] = to_row(rowbest[...])
-
-
-def low_kernel(l1, edge, unit, uh, u2, e1, e2, rowbest0, best0, hbest0, l2best, cbest, keys,
-               best, front, rear, cross, chip, hbest, l1best, u1, c1, c2, s, rowbest, nearbest):
+        at = jnp.where(me == 1, BELOW, 0)
+        d1[...] = columns(keys[pl.ds(at, 1), :])
+        d2[...] = columns(keys[pl.ds(at + 8, 1), :])
+
+
+def low_kernel(l1, edge, unit, uh, u2, c1, c2, e1, e2, rowbest0, best0, hbest0, l2best, cbest, keys,
+               best, front, rear, cross, chip, hbest, l1best, u1, s, rowbest, nearbest):
     me = lax.axis_index("row")
     odd = me % 2 == 1
     best[...], hbest[...] = best0[...], hbest0[...]
@@ -175,8 +178,6 @@
     @pl.when(me == 1)
     def _():
         normalise(l1, u1)
-        own = key_rows(keys, 0)
-        c1[...], c2[...] = columns(own[0]), columns(own[1])
         first = meet(unit, u1, 3, keys, c1, c2, s, rowbest)
         best[...] = jnp.maximum(best[...], to_row(rowbest[...]))
         nearbest[...] = rowbest0[...]
@@ -193,8 +194,6 @@
         def _():
             normalise(l1, u1)
 
-        low = key_rows(keys, -2)
-        c1[...], c2[...] = columns(low[0]), columns(low[1])
         for y, piece, out in ((unit, 0, best), (uh, 2, hbest)):
             out[...] = jnp.maximum(out[...], meet(u1, y, piece, keys, c1, c2, s, rowbest))
         l1best[...] = to_row(rowbest[...])
@@ -261,12 +260,12 @@
     best, cbest, u2, c1, c2, rowbest = call(
         near_kernel, [row] * 2 + [unit_] + [wide] * 3, [square], l2, unit, uc, best, cbest, keys
     )
-    uh, hbest, l2best, rowbest = call(
-        high_kernel, [unit_, row, row, wide], [square], h, u2, c1, c2, rowbest, keys
+    uh, hbest, l2best, rowbest, d1, d2 = call(
+        high_kernel, [unit_, row, row, wide, wide, wide], [square], h, u2, c1, c2, rowbest, keys
     )
     best, front, rear, cross, chip = call(
-        low_kernel, [row] * 5, [line, line, held, col, col, square, col, col],
-        l1, edge, unit, uh, u2, c1, c2, rowbest, best, hbest, l2best, cbest, keys,
+        low_kernel, [row] * 5, [line, line, held, square, col, col],
+        l1, edge, unit, uh, u2, d1, d2, c1, c2, rowbest, best, hbest, l2best, cbest, keys,
     )
     last = devices - 1
     far = [(i + j, i + j + 2) for i in range(0, devices - 2, 4) for j in range(2)]

time: 34.7 us -> 34.6 us (level)
  no operation moved by 1% of the time
where the time goes in v2:
time: 34.6 us; the launch traced here: 34.5 us
  starting transfers between devices  19.1 us (55%)
  waiting for transfers between devices  8.62 us (25%)
  Pallas kernels  6.03 us (17%)
  other arithmetic  0.59 us (2%)
    ppermute x8, starting transfers between devices, moved(): return lax.ppermute(x, 'row', pairs)  19.1 us
    ppermute x8, waiting for transfers between devices, moved(): return lax.ppermute(x, 'row', pairs)  8.62 us
    pallas_call x5, Pallas kernels, call(): pl.pallas_call(kernel, out_shape=outs, in_specs=[pl.BlockSpec(memory_spac...  6.03 us
  transfers between devices with their start and end apart: 8, of which 4 were waited for; matrix products, arithmetic and copies ran while one was open for 0% of the time, Pallas kernels for 14%

profile of v2, /device:TPU:37, one launch (start us, length us, event | category | flops | bytes accessed | tf_op | source)
XLA Modules:
  0.0 34.5 jit_solution(5694749519939368321)
XLA Ops:
  0.0 1.3 %collective-permute-start.1 = (bf16[512,512]{1,0:T(8,128)(2,1)}, bf16[512,512]{1,0:T(8,128)(2,1)S(1)}, u32[]{:S(2)}, u32[]{:S(2)}) collective-permute-start(bf16[512,512]{1,0:T(8,128)(2,1)} %own_.1), channel_id=1, source_target_pairs={{2,1},{4,6},{66,65},{68,70},{130,129},{132,134},{194,193},{196,198}} | collective-permute-start | bytes 1572872 | tf_op jit(solution)/shard_map/ppermute | solution.py:18
  1.3 1.3 %collective-permute-start.3 = (bf16[512,512]{1,0:T(8,128)(2,1)}, bf16[512,512]{1,0:T(8,128)(2,1)S(1)}, u32[]{:S(2)}, u32[]{:S(2)}) collective-permute-start(bf16[512,512]{1,0:T(8,128)(2,1)} %own_.1), channel_id=1, source_target_pairs={{0,1},{2,3},{3,4},{4,5},{5,6},{6,7},{7,8},{8,9},{9,10},{10,11},{11... | collective-permute-start | bytes 1572872 | tf_op jit(solution)/shard_map/ppermute | solution.py:18
  2.6 1.3 %collective-permute-start.2 = (bf16[512,512]{1,0:T(8,128)(2,1)}, bf16[512,512]{1,0:T(8,128)(2,1)S(1)}, u32[]{:S(2)}, u32[]{:S(2)}) collective-permute-start(bf16[512,512]{1,0:T(8,128)(2,1)} %own_.1), channel_id=1, source_target_pairs={{3,1},{5,3},{6,4},{7,5},{8,6},{9,7},{10,8},{11,9},{12,10},{13,11},... | collective-permute-start | bytes 1572872 | tf_op jit(solution)/shard_map/ppermute | solution.py:18
  3.9 11.0 %collective-permute-start = (bf16[512,512]{1,0:T(8,128)(2,1)}, bf16[512,512]{1,0:T(8,128)(2,1)S(1)}, u32[]{:S(2)}, u32[]{:S(2)}) collective-permute-start(bf16[512,512]{1,0:T(8,128)(2,1)} %own_.1), channel_id=1, source_target_pairs={{1,3},{2,4},{3,5},{4,1},{5,7},{6,8},{7,9},{8,10},{9,11},{10,12},{1... | collective-permute-start | bytes 1572872 | tf_op jit(solution)/shard_map/ppermute | solution.py:18
  14.9 2.0 %shard_map.37 = (bf16[512,512]{1,0:T(8,128)(2,1)S(1)}, f32[1,512]{1,0:T(1,128)S(1)}, f32[16,512]{1,0:T(8,128)S(1)}) custom-call(bf16[512,512]{1,0:T(8,128)(2,1)} %own_.1, s32[1,128]{1,0:T(1,128)} %bitcast.4, s32[256,128]{1,0:T(8,128)} %bitcast.3), custom_call_target="tpu_custom_call" | custom-call | tf_op jit(solution)/shard_map/pallas_call | solution.py:215
  16.9 0.0 collective-permute-done.1.c.edge
  16.9 0.8 %shard_map.38 = (bf16[512,512]{1,0:T(8,128)(2,1)S(1)}, f32[1,512]{1,0:T(1,128)S(1)}, f32[1,512]{1,0:T(1,128)S(1)}) custom-call(bf16[512,512]{1,0:T(8,128)(2,1)S(1)} %collective-permute-done.1.c.edge, bf16[512,512]{1,0:T(8,128)(2,1)S(1)} %get-tuple-element.28.unit, f32[1,512]{1,0:T(1,128)S(1)} %get-tuple-element.29.best0, f32[16,512]{1,0:T(8,128)S(1)} %get-tuple-element.30.keys), custom_call_target="tpu_custom_call" | custom-call | tf_op jit(solution)/shard_map/pallas_call | solution.py:215
  17.7 6.4 %collective-permute-done.3.l2 = bf16[512,512]{1,0:T(8,128)(2,1)S(1)} collective-permute-done((bf16[512,512]{1,0:T(8,128)(2,1)}, bf16[512,512]{1,0:T(8,128)(2,1)S(1)}, u32[]{:S(2)}, u32[]{:S(2)}) %collective-permute-start.3) | collective-permute-done | bytes 524320 | tf_op jit(solution)/shard_map/ppermute | solution.py:18
  24.0 1.4 %shard_map.39 = (f32[1,512]{1,0:T(1,128)S(1)}, f32[1,512]{1,0:T(1,128)S(1)}, bf16[512,512]{1,0:T(8,128)(2,1)S(1)}, f32[512,128]{1,0:T(8,128)S(1)}, f32[512,128]{1,0:T(8,128)S(1)}, /*index=5*/f32[512,128]{1,0:T(8,128)S(1)}) custom-call(bf16[512,512]{1,0:T(8,128)(2,1)S(1)} %collective-permute-done.3.l2, bf16[512,512]{1,0:T(8,128)(2,1)S(1)} %get-tuple-element.28.unit, ...), custom_call_target="tpu_custom_call" | custom-call | tf_op jit(solution)/shard_map/pallas_call | solution.py:215
  25.5 0.0 collective-permute-done.2.h
  25.5 0.8 %shard_map.40 = (bf16[512,512]{1,0:T(8,128)(2,1)S(1)}, f32[1,512]{1,0:T(1,128)S(1)}, f32[1,512]{1,0:T(1,128)S(1)}, f32[512,128]{1,0:T(8,128)S(1)}, f32[512,128]{1,0:T(8,128)S(1)}, /*index=5*/f32[512,128]{1,0:T(8,128)S(1)}) custom-call(bf16[512,512]{1,0:T(8,128)(2,1)S(1)} %collective-permute-done.2.h, bf16[512,512]{1,0:T(8,128)(2,1)S(1)} %get-tuple-element.34.u2, ...), custom_call_target="tpu_custom_call" | custom-call | tf_op jit(solution)/shard_map/pallas_call | solution.py:215
  26.3 0.3 collective-permute-done.l1
  26.5 1.1 %shard_map.41 = (f32[1,512]{1,0:T(1,128)S(1)}, f32[1,512]{1,0:T(1,128)S(1)}, f32[1,512]{1,0:T(1,128)S(1)}, f32[1,512]{1,0:T(1,128)S(1)}, f32[1,512]{1,0:T(1,128)S(1)}) custom-call(bf16[512,512]{1,0:T(8,128)(2,1)S(1)} %collective-permute-done.l1, bf16[512,512]{1,0:T(8,128)(2,1)S(1)} %collective-permute-done.1.c.edge, ...), custom_call_target="tpu_custom_call" | custom-call | tf_op jit(solution)/shard_map/pallas_call | solution.py:215
  27.6 0.2 collective-permute-start.4
  27.8 3.6 %collective-permute-start.5 = (f32[1,512]{1,0:T(1,128)S(1)}, f32[1,512]{1,0:T(1,128)S(1)}, u32[]{:S(2)}, u32[]{:S(2)}) collective-permute-start(f32[1,512]{1,0:T(1,128)S(1)} %get-tuple-element.48), channel_id=1, source_target_pairs={{1,4},{4,2},{2,0},{0,1},{3,5},{6,8},{7,9},{10,12},{11,13},{14,16},... | collective-permute-start | bytes 6152 | tf_op jit(solution)/shard_map/ppermute | solution.py:18
  31.4 0.4 %collective-permute-start.6 = (f32[1,512]{1,0:T(1,128)S(1)}, f32[1,512]{1,0:T(1,128)S(1)}, u32[]{:S(2)}, u32[]{:S(2)}) collective-permute-start(f32[1,512]{1,0:T(1,128)S(1)} %get-tuple-element.49), channel_id=1, source_target_pairs={{0,2},{1,3},{4,6},{5,7},{8,10},{9,11},{12,14},{13,15},{16,18},{17,... | collective-permute-start | bytes 6152 | tf_op jit(solution)/shard_map/ppermute | solution.py:18
  31.9 0.0 collective-permute-start.7
  31.9 0.0 collective-permute-done.4
  31.9 0.3 collective-permute-done.5
  32.2 1.7 %collective-permute-done.6 = f32[1,512]{1,0:T(1,128)S(1)} collective-permute-done((f32[1,512]{1,0:T(1,128)S(1)}, f32[1,512]{1,0:T(1,128)S(1)}, u32[]{:S(2)}, u32[]{:S(2)}) %collective-permute-start.6) | collective-permute-done | bytes 2080 | tf_op jit(solution)/shard_map/ppermute | solution.py:18
  33.9 0.0 collective-permute-done.7
  33.9 0.6 %maximum_maximum_fusion = f32[1,512]{1,0:T(1,128)} fusion(f32[1,512]{1,0:T(1,128)S(1)} %collective-permute-done.7, f32[1,512]{1,0:T(1,128)S(1)} %collective-permute-done.6, f32[1,512]{1,0:T(1,128)S(1)} %collective-permute-done.5, f32[1,512]{1,0:T(1,128)S(1)} %get-tuple-element.46, f32[1,512]{1,0:T(1,128)S(1)} %collective-permute-done.4), kind=kLoop, calls=%fused_computation | loop fusion | flops 2048 | bytes 12288 | tf_op jit(solution)/shard_map/max | solution.py:283
Async XLA Ops:
  0.0 16.9 %collective-permute-start.1 = (bf16[512,512]{1,0:T(8,128)(2,1)}, bf16[512,512]{1,0:T(8,128)(2,1)S(1)}, u32[]{:S(2)}, u32[]{:S(2)}) collective-permute-start(bf16[512,512]{1,0:T(8,128)(2,1)} %own_.1), channel_id=1, source_target_pairs={{2,1},{4,6},{66,65},{68,70},{130,129},{132,134},{194,193},{196,198}} | collective-permute-start | bytes 1572872 | tf_op jit(solution)/shard_map/ppermute | solution.py:18
  1.3 22.7 %collective-permute-start.3 = (bf16[512,512]{1,0:T(8,128)(2,1)}, bf16[512,512]{1,0:T(8,128)(2,1)S(1)}, u32[]{:S(2)}, u32[]{:S(2)}) collective-permute-start(bf16[512,512]{1,0:T(8,128)(2,1)} %own_.1), channel_id=1, source_target_pairs={{0,1},{2,3},{3,4},{4,5},{5,6},{6,7},{7,8},{8,9},{9,10},{10,11},{11... | collective-permute-start | bytes 1572872 | tf_op jit(solution)/shard_map/ppermute | solution.py:18
  2.6 22.8 %collective-permute-start.2 = (bf16[512,512]{1,0:T(8,128)(2,1)}, bf16[512,512]{1,0:T(8,128)(2,1)S(1)}, u32[]{:S(2)}, u32[]{:S(2)}) collective-permute-start(bf16[512,512]{1,0:T(8,128)(2,1)} %own_.1), channel_id=1, source_target_pairs={{3,1},{5,3},{6,4},{7,5},{8,6},{9,7},{10,8},{11,9},{12,10},{13,11},... | collective-permute-start | bytes 1572872 | tf_op jit(solution)/shard_map/ppermute | solution.py:18
  3.9 22.6 %collective-permute-start = (bf16[512,512]{1,0:T(8,128)(2,1)}, bf16[512,512]{1,0:T(8,128)(2,1)S(1)}, u32[]{:S(2)}, u32[]{:S(2)}) collective-permute-start(bf16[512,512]{1,0:T(8,128)(2,1)} %own_.1), channel_id=1, source_target_pairs={{1,3},{2,4},{3,5},{4,1},{5,7},{6,8},{7,9},{8,10},{9,11},{10,12},{1... | collective-permute-start | bytes 1572872 | tf_op jit(solution)/shard_map/ppermute | solution.py:18
  27.6 4.2 %collective-permute-start.4 = (f32[1,512]{1,0:T(1,128)S(1)}, f32[1,512]{1,0:T(1,128)S(1)}, u32[]{:S(2)}, u32[]{:S(2)}) collective-permute-start(f32[1,512]{1,0:T(1,128)S(1)} %get-tuple-element.47), channel_id=1, source_target_pairs={{1,2},{2,0},{0,1},{62,61},{61,63},{63,62},{3,4},{5,6},{7,8},{9,10}... | collective-permute-start | bytes 6152 | tf_op jit(solution)/shard_map/ppermute | solution.py:18
  27.8 4.4 %collective-permute-start.5 = (f32[1,512]{1,0:T(1,128)S(1)}, f32[1,512]{1,0:T(1,128)S(1)}, u32[]{:S(2)}, u32[]{:S(2)}) collective-permute-start(f32[1,512]{1,0:T(1,128)S(1)} %get-tuple-element.48), channel_id=1, source_target_pairs={{1,4},{4,2},{2,0},{0,1},{3,5},{6,8},{7,9},{10,12},{11,13},{14,16},... | collective-permute-start | bytes 6152 | tf_op jit(solution)/shard_map/ppermute | solution.py:18
  31.4 2.4 %collective-permute-start.6 = (f32[1,512]{1,0:T(1,128)S(1)}, f32[1,512]{1,0:T(1,128)S(1)}, u32[]{:S(2)}, u32[]{:S(2)}) collective-permute-start(f32[1,512]{1,0:T(1,128)S(1)} %get-tuple-element.49), channel_id=1, source_target_pairs={{0,2},{1,3},{4,6},{5,7},{8,10},{9,11},{12,14},{13,15},{16,18},{17,... | collective-permute-start | bytes 6152 | tf_op jit(solution)/shard_map/ppermute | solution.py:18
  31.9 2.0 %collective-permute-start.7 = (f32[1,512]{1,0:T(1,128)S(1)}, f32[1,512]{1,0:T(1,128)S(1)}, u32[]{:S(2)}, u32[]{:S(2)}) collective-permute-start(f32[1,512]{1,0:T(1,128)S(1)} %get-tuple-element.50), channel_id=1, source_target_pairs={{0,1},{2,3},{4,5},{6,7},{8,9},{10,11},{12,13},{14,15},{16,17},{18,... | collective-permute-start | bytes 6152 | tf_op jit(solution)/shard_map/ppermute | solution.py:18
